TPU v7x, 32 devices: a whole 2x2x4 slice. The times are simulated.
32 devices in a mesh: grid: 4 (over y, x), fsdp: 8 (over z, core).
Axes of the slice: x: 2, y: 2, z: 4, core: 2. Of those that a mesh axis runs over, the one named last changes fastest.
Arguments:
- hidden: bfloat16 [512, 4096], P('fsdp'), may hold values from -16 to 16
- norm_gain: float32 [4096], replicated, may hold values from 0.5 to 1.5
- base_head: bfloat16 [8192, 4096], P('fsdp'), may hold values from -1 to 1
- first_dir: bfloat16 [8192, 4096], P('fsdp'), may hold values from -0.09375 to 0.09375
- second_dir: bfloat16 [8192, 4096], P('fsdp'), may hold values from -0.09375 to 0.09375
- coords: int32 [8, 2], P('grid'), parts along dimension 0, may hold values from 0 to 7
- targets: int32 [512], replicated, may hold values from 0 to 8191
Outputs:
- token_loss: float32 [8, 512], P('grid', 'fsdp'), parts along dimension 0
- mean_loss: float32 [8], P('grid'), parts along dimension 0
There are 4 independent parts, one for each index of `grid`. A program takes and returns all parts, laid end to end along the dimension named above; an argument that names none is the same for every part. Nothing has to cross between parts.
All inputs are finite; a program needn't handle non-finite values.
Results may differ from a plain program's by a relative error of at most 0.0003.
Values may be sent and summed in bfloat16 or wider, within the bound.
A program may use at most 128 MiB of HBM per device.

v0:
```python
import jax
import jax.numpy as jnp
from jax import lax
from jax.sharding import PartitionSpec as P

epsilon = 1e-05


def combined_all(part, axis, combine):
    gathered = jax.tree.map(lambda a: lax.all_gather(a, axis), part)

    def take(source):
        return jax.tree.map(lambda a: lax.dynamic_index_in_dim(a, source, 0, False), gathered)

    return lax.fori_loop(
        1, lax.axis_size(axis), lambda source, state: combine(state, take(source)), take(0)
    )


def mixing_of(coords):
    levels = jnp.arange(8, dtype=jnp.int32)
    level_table = (2.0 * levels.astype(jnp.float32) - 7.0) / 7.0
    chosen = (coords[:, :, None] == levels[None, None, :]).astype(jnp.float32)
    return jnp.sum(chosen * level_table, axis=2)


def rms_normalize(rows_in, norm_gain):
    widened = rows_in.astype(jnp.float32)
    inv_rms = lax.rsqrt(jnp.mean(widened * widened, axis=1, keepdims=True) + epsilon)
    return (widened * inv_rms * norm_gain).astype(jnp.bfloat16)


def combine(earlier, later):
    row_top = jnp.maximum(earlier[0], later[0])
    exp_sums = earlier[1] * jnp.exp(earlier[0] - row_top) + later[1] * jnp.exp(later[0] - row_top)
    return (row_top, exp_sums, earlier[2] + later[2])


def body(hidden, norm_gain, base_head, first_dir, second_dir, coords, targets):
    mixing = mixing_of(coords)
    rebuilt = []
    for point_idx in range(coords.shape[0]):
        summed = (
            base_head.astype(jnp.float32)
            + mixing[point_idx, 0] * first_dir.astype(jnp.float32)
            + mixing[point_idx, 1] * second_dir.astype(jnp.float32)
        )
        rebuilt.append(summed.astype(jnp.bfloat16))
    head_rows = jnp.stack(rebuilt)
    normed = rms_normalize(hidden, norm_gain)
    logits = jnp.einsum(
        "pvd,td->ptv",
        head_rows,
        lax.all_gather(normed, "fsdp", axis=0, tiled=True),
        preferred_element_type=jnp.float32,
    )
    own_count = hidden.shape[0]
    vocab_count = base_head.shape[0]
    shard_idx = lax.axis_index("fsdp")
    target_col = targets - shard_idx * vocab_count
    columns = jnp.arange(vocab_count, dtype=jnp.int32)
    matches = target_col[:, None] == columns[None, :]
    picked = jnp.sum(jnp.where(matches[None, :, :], logits, 0.0), axis=2)
    local_top = jnp.max(logits, axis=2)
    exp_sums = jnp.sum(jnp.exp(logits - local_top[:, :, None]), axis=2)
    row_top, all_sums, all_picked = combined_all((local_top, exp_sums, picked), "fsdp", combine)
    all_loss = row_top + jnp.log(all_sums) - all_picked
    token_loss = lax.dynamic_slice_in_dim(all_loss, shard_idx * own_count, own_count, 1)
    mean_loss = jnp.mean(all_loss, axis=1)
    return (token_loss, mean_loss)


def solution(mesh):
    placed = (
        P("fsdp", None),
        P(),
        P("fsdp", None),
        P("fsdp", None),
        P("fsdp", None),
        P("grid", None),
        P(),
    )
    return jax.shard_map(
        body, mesh=mesh, in_specs=placed, out_specs=(P("grid", "fsdp"), P("grid")), check_vma=False
    )
```

profile of v0, /device:TPU:0, one launch (start us, length us, event | category | flops | bytes accessed | tf_op | source)
XLA Modules:
  0.0 125.8 jit_solution(17976411452856553124)
XLA Ops:
  7.2 0.0 all-gather.8.cloned.1.call-start
  7.2 1.2 fusion.16
  8.5 2.0 %fusion.18 = bf16[64,4096]{1,0:T(8,128)(2,1)} fusion(bf16[64,4096]{1,0:T(8,128)(2,1)} %param.9, f32[4096]{0:T(1024)} %param.10, f32[64]{0:T(128)S(1)} %add_rsqrt_fusion), kind=kLoop, calls=%fused_computation.34 | loop fusion | flops 1048576 | bytes 1065216 | tf_op jit(solution)/shard_map/convert_element_type | solution.py:30
  10.5 0.0 all-gather.8.cloned.1.call-update
  10.5 0.8 fusion.19
  11.4 0.7 fusion.22
  12.0 0.7 broadcast_subtract_fusion
  12.7 0.4 iota_compare_fusion
  13.1 18.8 %fusion.11 = (bf16[1,1024,4096]{2,1,0:T(8,128)(2,1)}, bf16[1,1024,4096]{2,1,0:T(8,128)(2,1)}) fusion(bf16[1024,4096]{1,0:T(8,128)(2,1)} %param.13, bf16[1024,4096]{1,0:T(8,128)(2,1)} %param.12, bf16[1024,4096]{1,0:T(8,128)(2,1)} %param.11, f32[]{:T(128)} %bitcast.5, f32[]{:T(128)} %bitcast.4, f32[]{:T(128)} %bitcast.8, f32[]{:T(128)} %bitcast.7), kind=kLoop, calls=%fused_computation.21 | loop fusion | flops 54525952 | bytes 41943056 | tf_op jit(solution)/shard_map/stack | solution.py:49
  31.8 28.4 %all-gather.8.cloned.1.call-done = bf16[512,4096]{1,0:T(8,128)(2,1)} async-done(((bf16[64,4096]{1,0:T(8,128)(2,1)}), bf16[512,4096]{1,0:T(8,128)(2,1)}) %all-gather.8.cloned.1.call-update) | async-done | bytes 4194320 | tf_op jit(solution)/shard_map/all_gather | solution.py:54
  60.3 13.4 %bitcast_reduce_fusion = (f32[2,512]{1,0:T(2,128)S(1)}, f32[512,2,1024]{2,0,1:T(8,128)S(1)}) fusion(bf16[1,1024,4096]{2,1,0:T(8,128)(2,1)} %get-tuple-element.205, bf16[1,1024,4096]{2,1,0:T(8,128)(2,1)} %get-tuple-element.204, bf16[512,4096]{1,0:T(8,128)(2,1)} %all-gather.8.cloned.1.call-done), kind=kOutput, calls=%fused_computation.24 | convolution fusion | flops 8624536576 | bytes 25169920 | tf_op jit(solution)/shard_map/pvd,td->ptv/dot_general | solution.py:51
  73.7 1.4 %fusion.14 = (f32[2,512]{1,0:T(2,128)S(1)}, f32[2,512]{1,0:T(2,128)S(1)}) fusion(f32[512,2,1024]{2,0,1:T(8,128)S(1)} %get-tuple-element.211, pred[512,1024]{1,0:T(8,128)(4,1)S(1)} %iota_compare_fusion, f32[2,512]{1,0:T(2,128)S(1)} %get-tuple-element.210), kind=kLoop, calls=%fused_computation.27 | loop fusion | flops 4192256 | bytes 4730880 | tf_op jit(solution)/shard_map/reduce_sum | solution.py:63
  75.1 14.1 %all-gather.5 = f32[8,2,512]{2,1,0:T(2,128)S(1)} all-gather(f32[1,2,512]{2,1,0:T(2,128)S(1)} %bitcast.50), channel_id=4, replica_groups=mesh['grid'=4,'fsdp'=8] {'fsdp'}, dimensions={0}, use_global_device_ids=true | all-gather | bytes 36864 | tf_op jit(solution)/shard_map/all_gather | solution.py:10
  89.2 14.1 %all-gather.4 = f32[8,2,512]{2,1,0:T(2,128)S(1)} all-gather(f32[1,2,512]{2,1,0:T(2,128)S(1)} %bitcast.49), channel_id=3, replica_groups=mesh['grid'=4,'fsdp'=8] {'fsdp'}, dimensions={0}, use_global_device_ids=true | all-gather | bytes 36864 | tf_op jit(solution)/shard_map/all_gather | solution.py:10
  103.3 14.1 %all-gather.3 = f32[8,2,512]{2,1,0:T(2,128)S(1)} all-gather(f32[1,2,512]{2,1,0:T(2,128)S(1)} %bitcast.48), channel_id=2, replica_groups=mesh['grid'=4,'fsdp'=8] {'fsdp'}, dimensions={0}, use_global_device_ids=true | all-gather | bytes 36864 | tf_op jit(solution)/shard_map/all_gather | solution.py:10
  117.4 0.3 while.19
  117.7 0.1 fusion.21
  117.8 0.5 broadcast_multiply_fusion
  118.4 0.6 constant_dynamic-slice_fusion
  (12 shorter events, 0.2 us)
Async XLA Ops:
  7.2 53.1 %all-gather.8.cloned.1.call-start = ((), (), s32[]{:S(2)}) async-start(), calls=%async_computation | async-start | bytes 4718592 | tf_op jit(solution)/shard_map/all_gather | solution.py:54
Sparse Core Ops, SparseCore 0:
  10.7 49.5 all-gather.7
where the time goes:
time: 126 us
  blocking collectives  42.2 us (33%)
  waiting for transfers between devices  28.5 us (23%)
  other arithmetic  26.2 us (21%)
  between operations  14.1 us (11%)
  matrix products  13.4 us (11%)
  local copies, waits for them, and re-layouts  1.29 us (1%)
    all_gather x3, blocking collectives, combined_all(): gathered = jax.tree.map(lambda a: lax.all_gather(a, axis), part)  42.2 us
    all_gather x1, waiting for transfers between devices, body(): lax.all_gather(normed, 'fsdp', axis=0, tiled=True)  28.4 us
    another operation x1, other arithmetic, body(): head_rows = jnp.stack(rebuilt)  18.8 us
    dot_general x1, matrix products, body(): jnp.einsum('pvd,td->ptv', head_rows, lax.all_gather(normed, 'fsdp', axis=...  13.4 us
  transfers between devices with their start and end apart: 1, of which 1 were waited for; matrix products, arithmetic and copies ran while one was open for 17% of the time, Pallas kernels for 0%

commit v1 on v0

v1 whole, which is shorter than its diff:
```python
import functools

import jax
import jax.numpy as jnp
from jax import lax
from jax.experimental import pallas as pl
from jax.experimental.pallas import tpu as pltpu
from jax.sharding import PartitionSpec as P

epsilon = 1e-05
MESH = pl.DeviceIdType.MESH
NUM_PIECES = 16
ROW_CHUNK = 32


def kernel(
    n_grid, n_fsdp, total_tokens,
    coords_ref, hidden_ref, gain_ref, targets_ref, base_ref, first_ref, second_ref,
    token_ref, mean_ref,
    w_buf, x_buf, acc, mix_own, mix_all, stat_own, stat_all,
    w_sem, up_sem, dn_sem, pt_sem, recv_sem, recv_pt_sem,
    mix_send, mix_recv, stat_send, stat_recv, known_sem,
):
    g = lax.axis_index("grid")
    f = lax.axis_index("fsdp")
    n_chips = n_fsdp // 2
    z, core = f // 2, f % 2
    n_all = n_grid * n_fsdp
    me = g * n_fsdp + f
    pts = coords_ref.shape[0]
    own, width = hidden_ref.shape
    vocab = base_ref.shape[0]
    kp = x_buf.shape[2]
    lanes = x_buf.shape[1]
    is_root = z == g
    go_up = jnp.logical_and(z >= g, z < n_chips - 1)
    go_dn = jnp.logical_and(z <= g, z > 0)

    def w_copy(j, p):
        src = (base_ref, first_ref, second_ref)[j]
        cols = pl.ds(pl.multiple_of(p * kp, kp), kp)
        return pltpu.make_async_copy(src.at[:, cols], w_buf.at[j, p], w_sem.at[j, p])

    barrier = pltpu.get_barrier_semaphore()
    for d in range(1, n_fsdp):
        pl.semaphore_signal(
            barrier, inc=1, device_id=(g, lax.rem(f + d, n_fsdp)), device_id_type=MESH
        )
    for d in range(1, n_grid):
        pl.semaphore_signal(
            barrier, inc=1, device_id=(lax.rem(g + d, n_grid), f), device_id_type=MESH
        )

    @pl.loop(0, NUM_PIECES)
    def _(p):
        for j in range(3):
            w_copy(j, p).start()

    for pt in range(pts):
        for k in range(2):
            level = jnp.full((1, lanes), coords_ref[pt, k], jnp.int32).astype(jnp.float32)
            mix_own[2 * pt + k : 2 * pt + k + 1, :] = (2.0 * level - 7.0) / 7.0
    mix_all[pl.ds(g, 1)] = mix_own[...][None]

    mine = pl.ds(pl.multiple_of(core * own, own), own)

    @pl.when(is_root)
    def _():
        squares = jnp.zeros((own, 1), jnp.float32)
        for p in range(NUM_PIECES):
            wide = hidden_ref[:, p * kp : (p + 1) * kp].astype(jnp.float32)
            squares = squares + jnp.sum(wide * wide, axis=1, keepdims=True)
        inv_rms = lax.rsqrt(squares / width + epsilon)
        for p in range(NUM_PIECES):
            wide = hidden_ref[:, p * kp : (p + 1) * kp].astype(jnp.float32)
            gain = gain_ref[:, p * kp : (p + 1) * kp]
            x_buf[p, mine, :] = (wide * inv_rms * gain).astype(jnp.bfloat16)

    pl.semaphore_wait(barrier, n_fsdp + n_grid - 2)

    def x_copy(p, send_sem, sem, target):
        return pltpu.make_async_remote_copy(
            src_ref=x_buf.at[p, mine], dst_ref=x_buf.at[p, mine],
            send_sem=send_sem.at[p], recv_sem=sem.at[p],
            device_id=(g, target), device_id_type=MESH,
        )

    partner = f + 1 - 2 * core
    above = lax.rem(f + 2, n_fsdp)
    below = lax.rem(f + n_fsdp - 2, n_fsdp)

    def send_on(p):
        @pl.when(go_up)
        def _():
            x_copy(p, up_sem, recv_sem, above).start()

        @pl.when(go_dn)
        def _():
            x_copy(p, dn_sem, recv_sem, below).start()

        x_copy(p, pt_sem, recv_pt_sem, partner).start()

    @pl.when(is_root)
    def _():
        @pl.loop(0, NUM_PIECES)
        def _(p):
            send_on(p)

    def mix_copy(d):
        to = lax.rem(g + d, n_grid)
        return pltpu.make_async_remote_copy(
            src_ref=mix_own, dst_ref=mix_all.at[g],
            send_sem=mix_send.at[d - 1], recv_sem=mix_recv.at[g],
            device_id=(to, f), device_id_type=MESH,
        )

    for d in range(1, n_grid):
        pl.semaphore_signal(
            known_sem, inc=1, device_id=(lax.rem(g + d, n_grid), f), device_id_type=MESH
        )
        mix_copy(d).start()

    acc[...] = jnp.zeros_like(acc)

    @pl.loop(0, NUM_PIECES)
    def _(p):
        @pl.when(jnp.logical_not(is_root))
        def _():
            x_copy(p, up_sem, recv_sem, above).wait_recv()
            send_on(p)

        other = pl.ds(pl.multiple_of((1 - core) * own, own), own)
        pltpu.make_async_remote_copy(
            src_ref=x_buf.at[p, other], dst_ref=x_buf.at[p, other],
            send_sem=pt_sem.at[p], recv_sem=recv_pt_sem.at[p],
            device_id=(g, partner), device_id_type=MESH,
        ).wait_recv()
        for j in range(3):
            w_copy(j, p).wait()
            acc[j] += lax.dot_general(
                w_buf[j, p], x_buf[p], (((1,), (1,)), ((), ())),
                preferred_element_type=jnp.float32,
            )

    for d in range(1, n_grid):
        pltpu.make_async_remote_copy(
            src_ref=mix_own, dst_ref=mix_all.at[lax.rem(g + d, n_grid)],
            send_sem=mix_send.at[d - 1], recv_sem=mix_recv.at[lax.rem(g + d, n_grid)],
            device_id=(lax.rem(g + d, n_grid), f), device_id_type=MESH,
        ).wait_recv()

    n_pts = n_grid * pts
    coef = []
    for pt in range(n_pts):
        rows = [mix_all[pt // pts, 2 * (pt % pts) + k : 2 * (pt % pts) + k + 1, :] for k in range(2)]
        coef.append([jnp.broadcast_to(r, (8, lanes)) for r in rows])

    targets = targets_ref[pl.ds(g, 1), :] - f * vocab
    steps = vocab // ROW_CHUNK
    tall = ROW_CHUNK // 8

    def block(c):
        rows = pl.ds(pl.multiple_of(c * ROW_CHUNK, ROW_CHUNK), ROW_CHUNK)
        return [acc[j, rows, :].reshape(tall, 8, lanes) for j in range(3)]

    def mixed(parts, pt):
        return parts[0] + coef[pt][0][None] * parts[1] + coef[pt][1][None] * parts[2]

    sub = lax.broadcasted_iota(jnp.int32, (tall, 8, lanes), 0) * 8 + lax.broadcasted_iota(
        jnp.int32, (tall, 8, lanes), 1
    )

    def top_step(c, carry):
        tops, picks = carry
        parts = block(c)
        hit = sub == (targets - c * ROW_CHUNK)[None]
        picks = tuple(
            pk + jnp.sum(jnp.where(hit, part, 0.0), axis=0) for pk, part in zip(picks, parts)
        )
        tops = tuple(
            jnp.maximum(tops[pt], jnp.max(mixed(parts, pt), axis=0)) for pt in range(n_pts)
        )
        return tops, picks

    low = jnp.full((8, lanes), -jnp.inf, jnp.float32)
    zero = jnp.zeros((8, lanes), jnp.float32)
    tops, picks = lax.fori_loop(0, steps, top_step, ((low,) * n_pts, (zero,) * 3))
    tops = [jnp.broadcast_to(jnp.max(t, axis=0, keepdims=True), (8, lanes)) for t in tops]
    picks = [jnp.sum(pk, axis=0, keepdims=True) for pk in picks]

    def sum_step(c, sums):
        parts = block(c)
        return tuple(
            sums[pt] + jnp.sum(jnp.exp(mixed(parts, pt) - tops[pt][None]), axis=0)
            for pt in range(n_pts)
        )

    sums = lax.fori_loop(0, steps, sum_step, (zero,) * n_pts)
    for pt in range(n_pts):
        at, row = pt // pts, pt % pts
        total = jnp.sum(sums[pt], axis=0, keepdims=True)
        stat_own[at, row : row + 1, :] = tops[pt][0:1] + jnp.log(total)
        stat_own[at, pts + row : pts + row + 1, :] = (
            picks[0] + coef[pt][0][0:1] * picks[1] + coef[pt][1][0:1] * picks[2]
        )
    stat_all[pl.ds(f, 1), pl.ds(g, 1)] = stat_own[pl.ds(g, 1)][None]

    @pl.loop(0, NUM_PIECES)
    def _(p):
        @pl.when(go_up)
        def _():
            x_copy(p, up_sem, recv_sem, above).wait_send()

        @pl.when(go_dn)
        def _():
            x_copy(p, dn_sem, recv_sem, below).wait_send()

        x_copy(p, pt_sem, recv_pt_sem, partner).wait_send()

    for d in range(1, n_grid):
        mix_copy(d).wait_send()
    pl.semaphore_wait(known_sem, n_grid - 1)

    def stat_copy(d):
        to = lax.rem(me + d, n_all)
        return pltpu.make_async_remote_copy(
            src_ref=stat_own.at[to // n_fsdp], dst_ref=stat_all.at[f, g],
            send_sem=stat_send.at[d - 1], recv_sem=stat_recv.at[me],
            device_id=(to // n_fsdp, lax.rem(to, n_fsdp)), device_id_type=MESH,
        )

    @pl.loop(1, n_all)
    def _(d):
        stat_copy(d).start()

    @pl.loop(1, n_all)
    def _(d):
        frm = lax.rem(me + d, n_all)
        fg, ff = frm // n_fsdp, lax.rem(frm, n_fsdp)
        pltpu.make_async_remote_copy(
            src_ref=stat_own.at[0], dst_ref=stat_all.at[ff, fg],
            send_sem=stat_send.at[d - 1], recv_sem=stat_recv.at[frm],
            device_id=(fg, ff), device_id_type=MESH,
        ).wait_recv()

    everything = jnp.zeros((pts, lanes), jnp.float32)
    chosen = jnp.zeros((pts, lanes), jnp.float32)
    for column in range(n_grid):
        here = stat_all[:, column]
        lse = here[:, :pts]
        top = jnp.max(lse, axis=0)
        loss = top + jnp.log(jnp.sum(jnp.exp(lse - top[None]), axis=0))
        loss = loss - jnp.sum(here[:, pts:], axis=0)
        everything = everything + loss
        chosen = jnp.where(z == column, loss, chosen)
    token_ref[...] = jnp.where(core == 0, chosen[:, :own], chosen[:, own:])
    for pt in range(pts):
        mean_ref[pt] = jnp.sum(everything[pt : pt + 1, :]) / total_tokens

    @pl.loop(1, n_all)
    def _(d):
        stat_copy(d).wait_send()


def body(n_grid, n_fsdp, hidden, norm_gain, base_head, first_dir, second_dir, coords, targets):
    own, width = hidden.shape
    vocab = base_head.shape[0]
    pts = coords.shape[0]
    total = targets.shape[0]
    lanes = total // n_grid
    assert lanes == 2 * own and n_fsdp == 2 * n_grid
    kp = width // NUM_PIECES
    n_all = n_grid * n_fsdp
    dma = pltpu.SemaphoreType.DMA
    vmem = pl.BlockSpec(memory_space=pltpu.VMEM)
    smem = pl.BlockSpec(memory_space=pltpu.SMEM)
    anywhere = pl.BlockSpec(memory_space=pl.ANY)
    token_loss, mean_loss = pl.pallas_call(
        functools.partial(kernel, n_grid, n_fsdp, total),
        out_shape=(
            jax.ShapeDtypeStruct((pts, own), jnp.float32),
            jax.ShapeDtypeStruct((pts,), jnp.float32),
        ),
        in_specs=[smem, vmem, vmem, vmem, anywhere, anywhere, anywhere],
        out_specs=(vmem, smem),
        scratch_shapes=[
            pltpu.VMEM((3, NUM_PIECES, vocab, kp), jnp.bfloat16),
            pltpu.VMEM((NUM_PIECES, lanes, kp), jnp.bfloat16),
            pltpu.VMEM((3, vocab, lanes), jnp.float32),
            pltpu.VMEM((2 * pts, lanes), jnp.float32),
            pltpu.VMEM((n_grid, 2 * pts, lanes), jnp.float32),
            pltpu.VMEM((n_grid, 2 * pts, lanes), jnp.float32),
            pltpu.VMEM((n_fsdp, n_grid, 2 * pts, lanes), jnp.float32),
            dma((3, NUM_PIECES)),
            dma((NUM_PIECES,)),
            dma((NUM_PIECES,)),
            dma((NUM_PIECES,)),
            dma((NUM_PIECES,)),
            dma((NUM_PIECES,)),
            dma((n_grid - 1,)),
            dma((n_grid,)),
            dma((n_all - 1,)),
            dma((n_all,)),
            pltpu.SemaphoreType.REGULAR,
        ],
        compiler_params=pltpu.CompilerParams(
            collective_id=0, has_side_effects=True, vmem_limit_bytes=60 * 1024 * 1024
        ),
    )(
        coords, hidden, norm_gain.reshape(1, width), targets.reshape(n_grid, lanes),
        base_head, first_dir, second_dir,
    )
    return (token_loss, mean_loss)


def solution(mesh):
    placed = (
        P("fsdp", None),
        P(),
        P("fsdp", None),
        P("fsdp", None),
        P("fsdp", None),
        P("grid", None),
        P(),
    )
    n_grid, n_fsdp = mesh.shape["grid"], mesh.shape["fsdp"]
    return jax.shard_map(
        functools.partial(body, n_grid, n_fsdp),
        mesh=mesh, in_specs=placed, out_specs=(P("grid", "fsdp"), P("grid")), check_vma=False,
    )
```

time: 126 us -> 62.1 us (0.49)
  Pallas kernels: 0 us -> 58.9 us
  blocking collectives: 42.2 us -> 0 us
  waiting for transfers between devices: 28.5 us -> 0 us
  other arithmetic: 26.2 us -> 0 us
  between operations: 14.1 us -> 0.64 us
  matrix products: 13.4 us -> 0 us
    pallas_call x0 -> x1, Pallas kernels: none -> 58.9 us  [body(): pl.pallas_call(functools.partial(kernel, n_grid, n_fsdp, total), out_shap...]
    all_gather x3 -> x0, blocking collectives: 42.2 us -> none  [combined_all(): gathered = jax.tree.map(lambda a: lax.all_gather(a, axis), part)]
    all_gather x1 -> x0, waiting for transfers between devices: 28.4 us -> none  [body(): lax.all_gather(normed, 'fsdp', axis=0, tiled=True)]
    another operation x1 -> x0, other arithmetic: 18.8 us -> none  [body(): head_rows = jnp.stack(rebuilt)]
    dot_general x1 -> x0, matrix products: 13.4 us -> none  [body(): jnp.einsum('pvd,td->ptv', head_rows, lax.all_gather(normed, 'fsdp', axis=...]
    reduce_sum x4 -> x0, other arithmetic: 3.63 us -> none  [the longest x1 1.42 us: body(): picked = jnp.sum(jnp.where(matches[None, :, :], logits, 0.0), axis=2)]
    unnamed x0 -> x2, local copies, waits for them, and re-layouts: none -> 2.36 us
    convert_element_type x1 -> x0, other arithmetic: 2.04 us -> none  [rms_normalize(): return (widened * inv_rms * norm_gain).astype(jnp.bfloat16)]
  transfers between devices with their start and end apart: 1 -> 0, of which waited for: 1 -> 0; matrix products, arithmetic and copies ran while one was open for 17% -> 0% of each run, Pallas kernels for 0% -> 0%
where the time goes in v1:
time: 62.1 us; the launch traced here: 61.9 us
  Pallas kernels  58.9 us (95%)
  local copies, waits for them, and re-layouts  2.36 us (4%)
  between operations  0.64 us (1%)
    pallas_call x1, Pallas kernels, body(): pl.pallas_call(functools.partial(kernel, n_grid, n_fsdp, total), out_shap...  58.9 us
    unnamed x2, local copies, waits for them, and re-layouts  2.36 us

profile of v1, /device:TPU:0, one launch (start us, length us, event | category | flops | bytes accessed | tf_op | source)
XLA Modules:
  0.0 61.9 jit_solution(16454447340841229636)
XLA Ops:
  0.6 58.9 %shard_map.86 = (f32[2,64]{1,0:T(2,128)}, f32[2]{0:T(128)}) custom-call(s32[2,2]{1,0:T(2,128)} %coords_ref.1, bf16[64,4096]{1,0:T(8,128)(2,1)} %hidden_ref.1, f32[1,4096]{1,0:T(1,128)} %bitcast.2, s32[4,128]{1,0:T(4,128)} %bitcast.3, bf16[1024,4096]{1,0:T(8,128)(2,1)} %base_ref.1, bf16[1024,4096]{1,0:T(8,128)(2,1)} %first_ref.1, bf16[1024,4096]{1,0:T(8,128)(2,1)} %second_ref.1), custom_call_target="tpu_custom_call" | custom-call | tf_op jit(solution)/shard_map/pallas_call | solution.py:278
  59.5 1.2 %copy.11 = f32[2,64]{1,0:T(2,128)} copy(f32[2,64]{1,0:T(2,128)} %get-tuple-element.4) | data formatting | bytes 1024
  60.8 1.1 %copy.12 = f32[2]{0:T(128)} copy(f32[2]{0:T(128)} %get-tuple-element.5) | data formatting | bytes 16

commit v2 on v1

--- a/solution.py
+++ b/solution.py
@@ -15,9 +15,9 @@
 
 def kernel(
     n_grid, n_fsdp, total_tokens,
-    coords_ref, hidden_ref, gain_ref, targets_ref, base_ref, first_ref, second_ref,
+    coords_ref, hidden_hbm, gain_ref, targets_ref, base_ref, first_ref, second_ref,
     token_ref, mean_ref,
-    w_buf, x_buf, acc, mix_own, mix_all, stat_own, stat_all,
+    hidden_ref, hidden_sem, w_buf, x_buf, acc, mix_own, mix_all, stat_own, stat_all,
     w_sem, up_sem, dn_sem, pt_sem, recv_sem, recv_pt_sem,
     mix_send, mix_recv, stat_send, stat_recv, known_sem,
 ):
@@ -28,7 +28,7 @@
     n_all = n_grid * n_fsdp
     me = g * n_fsdp + f
     pts = coords_ref.shape[0]
-    own, width = hidden_ref.shape
+    own, width = hidden_hbm.shape
     vocab = base_ref.shape[0]
     kp = x_buf.shape[2]
     lanes = x_buf.shape[1]
@@ -51,6 +51,10 @@
             barrier, inc=1, device_id=(lax.rem(g + d, n_grid), f), device_id_type=MESH
         )
 
+    @pl.when(is_root)
+    def _():
+        pltpu.make_async_copy(hidden_hbm, hidden_ref, hidden_sem).start()
+
     @pl.loop(0, NUM_PIECES)
     def _(p):
         for j in range(3):
@@ -66,6 +70,7 @@
 
     @pl.when(is_root)
     def _():
+        pltpu.make_async_copy(hidden_hbm, hidden_ref, hidden_sem).wait()
         squares = jnp.zeros((own, 1), jnp.float32)
         for p in range(NUM_PIECES):
             wide = hidden_ref[:, p * kp : (p + 1) * kp].astype(jnp.float32)
@@ -122,13 +127,7 @@
 
     acc[...] = jnp.zeros_like(acc)
 
-    @pl.loop(0, NUM_PIECES)
-    def _(p):
-        @pl.when(jnp.logical_not(is_root))
-        def _():
-            x_copy(p, up_sem, recv_sem, above).wait_recv()
-            send_on(p)
-
+    def compute(p):
         other = pl.ds(pl.multiple_of((1 - core) * own, own), own)
         pltpu.make_async_remote_copy(
             src_ref=x_buf.at[p, other], dst_ref=x_buf.at[p, other],
@@ -141,6 +140,19 @@
                 w_buf[j, p], x_buf[p], (((1,), (1,)), ((), ())),
                 preferred_element_type=jnp.float32,
             )
+
+    @pl.loop(0, NUM_PIECES)
+    def _(p):
+        @pl.when(jnp.logical_not(is_root))
+        def _():
+            x_copy(p, up_sem, recv_sem, above).wait_recv()
+            send_on(p)
+
+        @pl.when(p > 0)
+        def _():
+            compute(p - 1)
+
+    compute(NUM_PIECES - 1)
 
     for d in range(1, n_grid):
         pltpu.make_async_remote_copy(
@@ -281,9 +293,11 @@
             jax.ShapeDtypeStruct((pts, own), jnp.float32),
             jax.ShapeDtypeStruct((pts,), jnp.float32),
         ),
-        in_specs=[smem, vmem, vmem, vmem, anywhere, anywhere, anywhere],
+        in_specs=[smem, anywhere, vmem, vmem, anywhere, anywhere, anywhere],
         out_specs=(vmem, smem),
         scratch_shapes=[
+            pltpu.VMEM((own, width), jnp.bfloat16),
+            dma,
             pltpu.VMEM((3, NUM_PIECES, vocab, kp), jnp.bfloat16),
             pltpu.VMEM((NUM_PIECES, lanes, kp), jnp.bfloat16),
             pltpu.VMEM((3, vocab, lanes), jnp.float32),

time: 62.1 us -> 47.7 us (0.77)
  Pallas kernels: 58.9 us -> 44.5 us
    pallas_call x1, Pallas kernels: 58.9 us -> 44.5 us  [body(): pl.pallas_call(functools.partial(kernel, n_grid, n_fsdp, total), out_shap...]
where the time goes in v2:
time: 47.7 us; the launch traced here: 47.5 us
  Pallas kernels  44.5 us (93%)
  local copies, waits for them, and re-layouts  2.36 us (5%)
  between operations  0.64 us (1%)
    pallas_call x1, Pallas kernels, body(): pl.pallas_call(functools.partial(kernel, n_grid, n_fsdp, total), out_shap...  44.5 us
    unnamed x2, local copies, waits for them, and re-layouts  2.36 us

profile of v2, /device:TPU:0, one launch (start us, length us, event | category | flops | bytes accessed | tf_op | source)
XLA Modules:
  0.0 47.5 jit_solution(1213673373331838761)
XLA Ops:
  0.6 44.5 %shard_map.86 = (f32[2,64]{1,0:T(2,128)}, f32[2]{0:T(128)}) custom-call(s32[2,2]{1,0:T(2,128)} %coords_ref.1, bf16[64,4096]{1,0:T(8,128)(2,1)} %hidden_hbm.1, f32[1,4096]{1,0:T(1,128)} %bitcast.2, s32[4,128]{1,0:T(4,128)} %bitcast.3, bf16[1024,4096]{1,0:T(8,128)(2,1)} %base_ref.1, bf16[1024,4096]{1,0:T(8,128)(2,1)} %first_ref.1, bf16[1024,4096]{1,0:T(8,128)(2,1)} %second_ref.1), custom_call_target="tpu_custom_call" | custom-call | tf_op jit(solution)/shard_map/pallas_call | solution.py:290
  45.2 1.2 %copy.11 = f32[2,64]{1,0:T(2,128)} copy(f32[2,64]{1,0:T(2,128)} %get-tuple-element.4) | data formatting | bytes 1024
  46.4 1.1 %copy.12 = f32[2]{0:T(128)} copy(f32[2]{0:T(128)} %get-tuple-element.5) | data formatting | bytes 16

commit v3 on v2

--- a/solution.py
+++ b/solution.py
@@ -16,7 +16,7 @@
 def kernel(
     n_grid, n_fsdp, total_tokens,
     coords_ref, hidden_hbm, gain_ref, targets_ref, base_ref, first_ref, second_ref,
-    token_ref, mean_ref,
+    packed_ref,
     hidden_ref, hidden_sem, w_buf, x_buf, acc, mix_own, mix_all, stat_own, stat_all,
     w_sem, up_sem, dn_sem, pt_sem, recv_sem, recv_pt_sem,
     mix_send, mix_recv, stat_send, stat_recv, known_sem,
@@ -55,10 +55,6 @@
     def _():
         pltpu.make_async_copy(hidden_hbm, hidden_ref, hidden_sem).start()
 
-    @pl.loop(0, NUM_PIECES)
-    def _(p):
-        for j in range(3):
-            w_copy(j, p).start()
 
     for pt in range(pts):
         for k in range(2):
@@ -125,6 +121,11 @@
         )
         mix_copy(d).start()
 
+    @pl.loop(0, NUM_PIECES)
+    def _(p):
+        for j in range(3):
+            w_copy(j, p).start()
+
     acc[...] = jnp.zeros_like(acc)
 
     def compute(p):
@@ -136,6 +137,7 @@
         ).wait_recv()
         for j in range(3):
             w_copy(j, p).wait()
+        for j in range(3):
             acc[j] += lax.dot_general(
                 w_buf[j, p], x_buf[p], (((1,), (1,)), ((), ())),
                 preferred_element_type=jnp.float32,
@@ -265,13 +267,21 @@
         loss = loss - jnp.sum(here[:, pts:], axis=0)
         everything = everything + loss
         chosen = jnp.where(z == column, loss, chosen)
-    token_ref[...] = jnp.where(core == 0, chosen[:, :own], chosen[:, own:])
+    packed_ref[:pts, :own] = jnp.where(core == 0, chosen[:, :own], chosen[:, own:])
     for pt in range(pts):
-        mean_ref[pt] = jnp.sum(everything[pt : pt + 1, :]) / total_tokens
+        mean = jnp.sum(everything[pt : pt + 1, :], axis=1, keepdims=True) / total_tokens
+        packed_ref[pts + pt : pts + pt + 1, :] = jnp.broadcast_to(mean, (1, lanes))
 
     @pl.loop(1, n_all)
     def _(d):
         stat_copy(d).wait_send()
+
+
+def split(packed_ref, token_ref, mean_ref):
+    pts, own = token_ref.shape
+    token_ref[...] = packed_ref[:pts, :own]
+    for pt in range(pts):
+        mean_ref[pt] = packed_ref[pts + pt, 0]
 
 
 def body(n_grid, n_fsdp, hidden, norm_gain, base_head, first_dir, second_dir, coords, targets):
@@ -287,14 +297,11 @@
     vmem = pl.BlockSpec(memory_space=pltpu.VMEM)
     smem = pl.BlockSpec(memory_space=pltpu.SMEM)
     anywhere = pl.BlockSpec(memory_space=pl.ANY)
-    token_loss, mean_loss = pl.pallas_call(
+    packed = pl.pallas_call(
         functools.partial(kernel, n_grid, n_fsdp, total),
-        out_shape=(
-            jax.ShapeDtypeStruct((pts, own), jnp.float32),
-            jax.ShapeDtypeStruct((pts,), jnp.float32),
-        ),
+        out_shape=jax.ShapeDtypeStruct((2 * pts, lanes), jnp.float32),
         in_specs=[smem, anywhere, vmem, vmem, anywhere, anywhere, anywhere],
-        out_specs=(vmem, smem),
+        out_specs=vmem,
         scratch_shapes=[
             pltpu.VMEM((own, width), jnp.bfloat16),
             dma,
@@ -324,7 +331,17 @@
         coords, hidden, norm_gain.reshape(1, width), targets.reshape(n_grid, lanes),
         base_head, first_dir, second_dir,
     )
-    return (token_loss, mean_loss)
+    return tuple(
+        pl.pallas_call(
+            split,
+            out_shape=(
+                jax.ShapeDtypeStruct((pts, own), jnp.float32),
+                jax.ShapeDtypeStruct((pts,), jnp.float32),
+            ),
+            in_specs=[vmem],
+            out_specs=(vmem, smem),
+        )(packed)
+    )
 
 
 def solution(mesh):

time: 47.7 us -> 40.6 us (0.85)
  Pallas kernels: 44.5 us -> 39.7 us
  local copies, waits for them, and re-layouts: 2.36 us -> 0 us
    pallas_call x1, Pallas kernels: 44.5 us -> 38.5 us  [body(): pl.pallas_call(functools.partial(kernel, n_grid, n_fsdp, total), out_shap...]
    unnamed x2 -> x0, local copies, waits for them, and re-layouts: 2.36 us -> none
    pallas_call x0 -> x1, Pallas kernels: none -> 1.26 us  [body(): pl.pallas_call(split, out_shape=(jax.ShapeDtypeStruct((pts, own), jnp.flo...]
where the time goes in v3:
time: 40.6 us; the launch traced here: 40.4 us
  Pallas kernels  39.7 us (98%)
  between operations  0.64 us (2%)
    pallas_call x1, Pallas kernels, body(): pl.pallas_call(functools.partial(kernel, n_grid, n_fsdp, total), out_shap...  38.5 us
    pallas_call x1, Pallas kernels, body(): pl.pallas_call(split, out_shape=(jax.ShapeDtypeStruct((pts, own), jnp.flo...  1.26 us

profile of v3, /device:TPU:0, one launch (start us, length us, event | category | flops | bytes accessed | tf_op | source)
XLA Modules:
  0.0 40.4 jit_solution(6378133307808348948)
XLA Ops:
  0.6 38.5 %shard_map.86.packed_ref = f32[4,128]{1,0:T(4,128)} custom-call(s32[2,2]{1,0:T(2,128)} %coords_ref.1, bf16[64,4096]{1,0:T(8,128)(2,1)} %hidden_hbm.1, f32[1,4096]{1,0:T(1,128)} %bitcast.2, s32[4,128]{1,0:T(4,128)} %bitcast.3, bf16[1024,4096]{1,0:T(8,128)(2,1)} %base_ref.1, bf16[1024,4096]{1,0:T(8,128)(2,1)} %first_ref.1, bf16[1024,4096]{1,0:T(8,128)(2,1)} %second_ref.1), custom_call_target="tpu_custom_call" | custom-call | tf_op jit(solution)/shard_map/pallas_call | solution.py:300
  39.1 1.3 %shard_map.87 = (f32[2,64]{1,0:T(2,128)}, f32[2]{0:T(128)}) custom-call(f32[4,128]{1,0:T(4,128)} %shard_map.86.packed_ref), custom_call_target="tpu_custom_call" | custom-call | tf_op jit(solution)/shard_map/pallas_call | solution.py:335

commit v4 on v3

--- a/solution.py
+++ b/solution.py
@@ -10,7 +10,7 @@
 epsilon = 1e-05
 MESH = pl.DeviceIdType.MESH
 NUM_PIECES = 16
-ROW_CHUNK = 32
+ROW_CHUNK = 64
 
 
 def kernel(

time: 40.6 us -> 40.4 us (level)
  no operation moved by 1% of the time
where the time goes in v4:
time: 40.4 us; the launch traced here: 40.1 us
  Pallas kernels  39.5 us (98%)
  between operations  0.64 us (2%)
    pallas_call x1, Pallas kernels, body(): pl.pallas_call(functools.partial(kernel, n_grid, n_fsdp, total), out_shap...  38.2 us
    pallas_call x1, Pallas kernels, body(): pl.pallas_call(split, out_shape=(jax.ShapeDtypeStruct((pts, own), jnp.flo...  1.26 us

profile of v4, /device:TPU:0, one launch (start us, length us, event | category | flops | bytes accessed | tf_op | source)
XLA Modules:
  0.0 40.1 jit_solution(11822176299209932188)
XLA Ops:
  0.6 38.2 %shard_map.86.packed_ref = f32[4,128]{1,0:T(4,128)} custom-call(s32[2,2]{1,0:T(2,128)} %coords_ref.1, bf16[64,4096]{1,0:T(8,128)(2,1)} %hidden_hbm.1, f32[1,4096]{1,0:T(1,128)} %bitcast.2, s32[4,128]{1,0:T(4,128)} %bitcast.3, bf16[1024,4096]{1,0:T(8,128)(2,1)} %base_ref.1, bf16[1024,4096]{1,0:T(8,128)(2,1)} %first_ref.1, bf16[1024,4096]{1,0:T(8,128)(2,1)} %second_ref.1), custom_call_target="tpu_custom_call" | custom-call | tf_op jit(solution)/shard_map/pallas_call | solution.py:300
  38.9 1.3 %shard_map.87 = (f32[2,64]{1,0:T(2,128)}, f32[2]{0:T(128)}) custom-call(f32[4,128]{1,0:T(4,128)} %shard_map.86.packed_ref), custom_call_target="tpu_custom_call" | custom-call | tf_op jit(solution)/shard_map/pallas_call | solution.py:335
